TPU v7x, 32 devices: a whole 2x2x4 slice. The times are simulated.
32 devices in a mesh: row: 8 (over z, core), col: 4 (over y, x).
Axes of the slice: x: 2, y: 2, z: 4, core: 2. Of those that a mesh axis runs over, the one named last changes fastest.
Arguments:
- gate_input: bfloat16 [2, 512, 53248], P(None, 'col', 'row'), may hold values from -6 to 6
- up_input: bfloat16 [2, 512, 53248], P(None, 'col', 'row'), may hold values from -6 to 6
- down_weight: bfloat16 [53248, 16384], P('row', 'col'), may hold values from -0.02734375 to 0.02734375
Outputs:
- mixed: bfloat16 [2, 512, 16384], P(None, 'row', 'col')
All inputs are finite; a program needn't handle non-finite values.
Results may differ from a plain program's by a relative error of at most 0.0049.
Values may be sent and summed in bfloat16 or wider, within the bound.
No kernel may reach another device: no remote copies, remote signals or barrier semaphores. Data moves between devices by JAX's collectives and lax.ppermute only.
A program may use at most 128 MiB of HBM per device.

v0:
```python
import jax
import jax.numpy as jnp
from jax import lax
from jax.sharding import PartitionSpec as P


def gated_hidden(gate_part, up_part):
    product = jax.nn.silu(gate_part.astype(jnp.float32)) * up_part.astype(jnp.float32)
    return product.astype(jnp.bfloat16)


def gathered_hidden(gate_part, up_part):
    return lax.all_gather(gated_hidden(gate_part, up_part), "col", axis=1, tiled=True)


def body(gate_input, up_input, down_weight):
    hidden_units = down_weight.shape[0]
    width = down_weight.shape[1]
    hidden = gathered_hidden(gate_input, up_input)
    seq_count = hidden.shape[0]
    seq_tokens = hidden.shape[1]
    flat = hidden.reshape(seq_count * seq_tokens, hidden_units)
    partial_value = jnp.dot(flat, down_weight, preferred_element_type=jnp.float32)
    partial_value = partial_value.reshape(seq_count, seq_tokens, width)
    mixed = lax.psum_scatter(partial_value, "row", scatter_dimension=1, tiled=True)
    return mixed.astype(jnp.bfloat16)


def solution(mesh):
    return jax.shard_map(
        body,
        mesh=mesh,
        in_specs=(P(None, "col", "row"), P(None, "col", "row"), P("row", "col")),
        out_specs=P(None, "row", "col"),
        check_vma=False,
    )
```

profile of v0, /device:TPU:0, one launch (start us, length us, event | category | flops | bytes accessed | tf_op | source)
XLA Modules:
  0.0 389.2 jit_solution(1998762316375179421)
XLA Ops:
  6.5 0.0 all-gather.2.cloned.1.call-start
  6.5 5.2 %fusion.6 = bf16[2,128,6656]{2,1,0:T(8,128)(2,1)} fusion(bf16[2,128,6656]{2,1,0:T(8,128)(2,1)} %param.4, bf16[2,128,6656]{2,1,0:T(8,128)(2,1)} %param.3), kind=kLoop, calls=%fused_computation.8 | loop fusion | flops 13631488 | bytes 10223616 | tf_op jit(solution)/shard_map/convert_element_type | solution.py:9
  11.7 0.0 all-gather.2.cloned.1.call-update
  11.7 0.0 reduce-scatter.2.cloned.1.call-start
  11.8 133.9 %all-gather.2.cloned.1.call-done = bf16[2,512,6656]{2,1,0:T(8,128)(2,1)} async-done(((bf16[2,128,6656]{2,1,0:T(8,128)(2,1)}), bf16[2,512,6656]{2,1,0:T(8,128)(2,1)}) %all-gather.2.cloned.1.call-update) | async-done | bytes 13631504 | tf_op jit(solution)/shard_map/all_gather | solution.py:13
  145.7 65.6 %fusion = f32[2,512,4096]{2,1,0:T(8,128)} fusion(bf16[2,512,6656]{2,1,0:T(8,128)(2,1)} %all-gather.2.cloned.1.call-done, bf16[6656,4096]{1,0:T(8,128)(2,1)} %param.5), kind=kOutput, calls=%fused_computation | convolution fusion | flops 55834574848 | bytes 84934656 | tf_op jit(solution)/shard_map/dot_general | solution.py:23
  211.3 0.0 reduce-scatter.2.cloned.1.call-update
  211.3 168.3 %reduce-scatter.2.cloned.1.call-done = f32[2,64,4096]{2,1,0:T(8,128)} async-done(((f32[2,512,4096]{2,1,0:T(8,128)}), f32[2,64,4096]{2,1,0:T(8,128)}) %reduce-scatter.2.cloned.1.call-update) | async-done | bytes 2097168 | tf_op jit(solution)/shard_map/reduce_scatter | solution.py:25
  379.7 2.7 convert_element_type.15
Async XLA Ops:
  6.5 139.2 %all-gather.2.cloned.1.call-start = ((), (), s32[]{:S(2)}) async-start(), calls=%async_computation.1 | async-start | bytes 17039360 | tf_op jit(solution)/shard_map/all_gather | solution.py:13
  11.7 367.9 %reduce-scatter.2.cloned.1.call-start = ((), (), s32[]{:S(2)}) async-start(), calls=%async_computation.2 | async-start | bytes 18874368 | tf_op jit(solution)/shard_map/reduce_scatter | solution.py:25
Sparse Core Ops, SparseCore 0:
  11.9 133.8 all-gather.1
  211.5 168.1 reduce-scatter.1
where the time goes:
time: 389 us
  waiting for transfers between devices  302 us (78%)
  matrix products  65.6 us (17%)
  between operations  13.4 us (3%)
  other arithmetic  7.86 us (2%)
    reduce_scatter x1, waiting for transfers between devices, body(): lax.psum_scatter(partial_value, 'row', scatter_dimension=1, tiled=True)  168 us
    all_gather x1, waiting for transfers between devices, gathered_hidden(): lax.all_gather(gated_hidden(gate_part, up_part), 'col', axis=1, tiled=True)  134 us
    dot_general x1, matrix products, body(): jnp.dot(flat, down_weight, preferred_element_type=jnp.float32)  65.6 us
  transfers between devices with their start and end apart: 2, of which 2 were waited for; matrix products, arithmetic and copies ran while one was open for 0% of the time, Pallas kernels for 0%

commit v1 on v0

v1 whole, which is shorter than its diff:
```python
import jax
import jax.numpy as jnp
from jax import lax
from jax.sharding import PartitionSpec as P


SIZES = (2, 3, 3)
LAST_CUTS = 2


def gated_hidden(gate_part, up_part):
    product = jax.nn.silu(gate_part.astype(jnp.float32)) * up_part.astype(jnp.float32)
    return product.astype(jnp.bfloat16)


def solution(mesh):
    n_row = mesh.shape["row"]
    n_col = mesh.shape["col"]
    share = n_row // n_col
    slow = 2 if n_col % 2 == 0 else 1
    fast = n_col // slow
    n = len(SIZES)

    def shift_slow(value, step):
        pairs = [(a * fast + b, (a + step) % slow * fast + b) for a in range(slow) for b in range(fast)]
        return lax.ppermute(value, "col", pairs)

    def shift_fast(value, step):
        pairs = [(a * fast + b, a * fast + (b + step) % fast) for a in range(slow) for b in range(fast)]
        return lax.ppermute(value, "col", pairs)

    def shift_part(value, step):
        pairs = [(z * share + k, z * share + (k + step) % share) for z in range(n_col) for k in range(share)]
        return lax.ppermute(value, "row", pairs)

    def shift_group(value, step):
        pairs = [(z * share + k, (z + step) % n_col * share + k) for z in range(n_col) for k in range(share)]
        return lax.ppermute(value, "row", pairs)

    def layer(gate_input, up_input, down_weight):
        seqs, tokens, units = gate_input.shape
        width = down_weight.shape[1]
        own = tokens // share
        rows = seqs * own
        half = units // 2
        row = lax.axis_index("row")
        col = lax.axis_index("col")
        group, part = row // share, row % share
        at_slow, at_fast = col // fast, col % fast
        edges = [rows * sum(SIZES[:i]) // sum(SIZES) for i in range(n + 1)]

        def place(source):
            return (at_slow - source // fast) % slow * fast + (at_fast - source % fast) % fast

        def hidden_of(lo, hi):
            hidden = gated_hidden(gate_input[:, :, lo:hi], up_input[:, :, lo:hi])
            hidden = hidden.reshape(seqs, share, own, hi - lo)
            return hidden.transpose(1, 0, 2, 3).reshape(share, rows, hi - lo)

        first = hidden_of(0, half)
        second = hidden_of(half, units)
        outs = {}
        for i in range(n):
            mine_first = first[:, edges[i]:edges[i + 1]]
            mine_second = second[:, edges[i]:edges[i + 1]]
            left, right = {(0, 0): mine_first}, {(0, 0): mine_second}
            for da in range(1, slow):
                left[da, 0] = shift_slow(mine_first, da)
            for db in range(1, fast):
                right[0, db] = shift_fast(mine_second, db)
            for da in range(slow):
                for db in range(fast):
                    if db:
                        left[da, db] = shift_fast(left[da, 0], db)
                    if da:
                        right[da, db] = shift_slow(right[0, db], da)
            order = [(da, db) for da in range(slow) for db in range(fast)]
            size = edges[i + 1] - edges[i]
            flat = jnp.concatenate([
                jnp.concatenate([left[at].reshape(share * size, half) for at in order], 0),
                jnp.concatenate([right[at].reshape(share * size, units - half) for at in order], 0),
            ], 1)
            cuts = LAST_CUTS if i == n - 1 else 1
            for j in range(cuts):
                lo, hi = width * j // cuts, width * (j + 1) // cuts
                sums = jnp.dot(flat, down_weight[:, lo:hi], preferred_element_type=jnp.float32).astype(jnp.bfloat16)
                sums = sums.reshape(n_col, share, size, hi - lo)
                total = lax.dynamic_index_in_dim(sums, part, 1, keepdims=False).astype(jnp.float32)
                for dk in range(1, share):
                    other = lax.dynamic_index_in_dim(sums, (part + dk) % share, 1, keepdims=False)
                    other = shift_part(other, dk)
                    total = total + other.astype(jnp.float32)
                total = total.astype(jnp.bfloat16)
                mine = lax.dynamic_index_in_dim(total, place(group), 0, keepdims=False).astype(jnp.float32)
                for dz in range(1, n_col):
                    block = lax.dynamic_index_in_dim(total, place((group + dz) % n_col), 0, keepdims=False)
                    block = shift_group(block, dz)
                    mine = mine + block.astype(jnp.float32)
                outs[i, j] = mine.astype(jnp.bfloat16)
        last = jnp.concatenate([outs[n - 1, j] for j in range(LAST_CUTS)], 1)
        whole = jnp.concatenate([outs[i, 0] for i in range(n - 1)] + [last], 0)
        return whole.reshape(seqs, own, width)

    return jax.shard_map(
        layer,
        mesh=mesh,
        in_specs=(P(None, "col", "row"), P(None, "col", "row"), P("row", "col")),
        out_specs=P(None, "row", "col"),
        check_vma=False,
    )
```

time: 389 us -> 263 us (0.68)
  the two profiles are of different devices: /device:TPU:0 before, /device:TPU:9 now
where the time goes in v1:
time: 263 us
  waiting for transfers between devices  120 us (46%)
  matrix products  95 us (36%)
  starting transfers between devices  35.7 us (14%)
  other arithmetic  8.15 us (3%)
  local copies, waits for them, and re-layouts  4.36 us (2%)
    dot_general x4, matrix products, layer(): jnp.dot(flat, down_weight[:, lo:hi], preferred_element_type=jnp.float32)  95 us
    ppermute x12, waiting for transfers between devices, shift_group(): return lax.ppermute(value, 'row', pairs)  76.2 us
    ppermute x9, waiting for transfers between devices, shift_fast(): return lax.ppermute(value, 'col', pairs)  23.4 us
    ppermute x9, waiting for transfers between devices, shift_slow(): return lax.ppermute(value, 'col', pairs)  19.9 us
    ppermute x12, starting transfers between devices, shift_group(): return lax.ppermute(value, 'row', pairs)  15.6 us
    ppermute x9, starting transfers between devices, shift_slow(): return lax.ppermute(value, 'col', pairs)  8.18 us
    ppermute x9, starting transfers between devices, shift_fast(): return lax.ppermute(value, 'col', pairs)  7.2 us
  transfers between devices with their start and end apart: 34, of which 15 were waited for; matrix products, arithmetic and copies ran while one was open for 39% of the time, Pallas kernels for 0%

profile of v1, /device:TPU:9, one launch (start us, length us, event | category | flops | bytes accessed | tf_op | source)
XLA Modules:
  0.0 263.1 jit_solution(13296769825180353483)
XLA Ops:
  0.0 4.0 %fusion.43 = (bf16[2,128,3328]{2,1,0:T(8,128)(2,1)S(1)}, bf16[2,128,3328]{2,1,0:T(8,128)(2,1)S(1)}) fusion(bf16[2,128,6656]{2,1,0:T(8,128)(2,1)} %param.4, bf16[2,128,6656]{2,1,0:T(8,128)(2,1)} %param.3), kind=kLoop, calls=%fused_computation.50 | loop fusion | flops 13631488 | bytes 10223616 | tf_op jit(solution)/shard_map/convert_element_type | solution.py:13
  4.2 1.3 collective-permute-start.3
  5.5 1.2 collective-permute-start.4
  10.5 4.5 %collective-permute-done.3 = bf16[2,32,3328]{2,1,0:T(8,128)(2,1)S(1)} collective-permute-done((bf16[2,32,3328]{2,1,0:T(8,128)(2,1)S(1)}, bf16[2,32,3328]{2,1,0:T(8,128)(2,1)S(1)}, u32[]{:S(2)}, u32[]{:S(2)}) %collective-permute-start.3) | collective-permute-done | bytes 426016 | tf_op jit(solution)/shard_map/ppermute | solution.py:30
  16.2 9.0 %collective-permute-done.1 = bf16[2,32,3328]{2,1,0:T(8,128)(2,1)} collective-permute-done((bf16[2,32,3328]{2,1,0:T(8,128)(2,1)S(1)}, bf16[2,32,3328]{2,1,0:T(8,128)(2,1)}, u32[]{:S(2)}, u32[]{:S(2)}) %collective-permute-start.1) | collective-permute-done | bytes 426016 | tf_op jit(solution)/shard_map/ppermute | solution.py:26
  25.4 1.2 collective-permute-start.5
  26.6 1.3 collective-permute-start.2
  27.9 10.9 %collective-permute-done.11 = bf16[2,48,3328]{2,1,0:T(8,128)(2,1)} collective-permute-done((bf16[2,48,3328]{2,1,0:T(8,128)(2,1)S(1)}, bf16[2,48,3328]{2,1,0:T(8,128)(2,1)}, u32[]{:S(2)}, u32[]{:S(2)}) %collective-permute-start.11) | collective-permute-done | bytes 639008 | tf_op jit(solution)/shard_map/ppermute | solution.py:26
  38.8 1.2 collective-permute-start.14
  40.3 11.3 %collective-permute-done.10 = bf16[2,48,3328]{2,1,0:T(8,128)(2,1)S(1)} collective-permute-done((bf16[2,48,3328]{2,1,0:T(8,128)(2,1)S(1)}, bf16[2,48,3328]{2,1,0:T(8,128)(2,1)S(1)}, u32[]{:S(2)}, u32[]{:S(2)}) %collective-permute-start.10) | collective-permute-done | bytes 639008 | tf_op jit(solution)/shard_map/ppermute | solution.py:30
  53.0 7.7 %collective-permute-done.2 = bf16[2,32,3328]{2,1,0:T(8,128)(2,1)} collective-permute-done((bf16[2,32,3328]{2,1,0:T(8,128)(2,1)}, bf16[2,32,3328]{2,1,0:T(8,128)(2,1)}, u32[]{:S(2)}, u32[]{:S(2)}) %collective-permute-start.2) | collective-permute-done | bytes 426016 | tf_op jit(solution)/shard_map/ppermute | solution.py:30
  61.9 24.1 %convolution_convert_fusion.1 = bf16[256,4096]{1,0:T(8,128)(2,1)S(1)} fusion(bf16[6656,4096]{1,0:T(8,128)(2,1)} %param.5, bf16[64,3328]{1,0:T(8,128)(2,1)} %bitcast.13, bf16[64,3328]{1,0:T(8,128)(2,1)} %bitcast.119, bf16[64,3328]{1,0:T(8,128)(2,1)} %bitcast.118, bf16[64,3328]{1,0:T(8,128)(2,1)} %bitcast.115, bf16[64,3328]{1,0:T(8,128)(2,1)} %bitcast.6, ...), kind=kOutput, calls=%fused_computation.5 | convolution fusion | flops 13986955264 | bytes 60030976 | tf_op jit(solution)/shard_map/dot_general | solution.py:86
  90.1 4.1 %collective-permute-start.6 = (bf16[4,32,4096]{2,1,0:T(8,128)(2,1)}, bf16[4,32,4096]{2,1,0:T(8,128)(2,1)}, u32[]{:S(2)}, u32[]{:S(2)}) collective-permute-start(bf16[4,32,4096]{2,1,0:T(8,128)(2,1)} %dynamic-slice_bitcast_fusion.1), channel_id=1, source_target_pairs={{0,4},{4,0},{8,12},{12,8},{16,20},{20,16},{24,28},{28,24},{1,5},{5... | collective-permute-start | bytes 3145736 | tf_op jit(solution)/shard_map/ppermute | solution.py:34
  94.2 32.7 %convolution_convert_fusion = bf16[384,4096]{1,0:T(8,128)(2,1)S(1)} fusion(bf16[6656,4096]{1,0:T(8,128)(2,1)} %param.5, bf16[96,3328]{1,0:T(8,128)(2,1)} %bitcast.28, bf16[96,3328]{1,0:T(8,128)(2,1)} %bitcast.27, bf16[96,3328]{1,0:T(8,128)(2,1)} %bitcast.26, bf16[96,3328]{1,0:T(8,128)(2,1)} %bitcast.114, bf16[96,3328]{1,0:T(8,128)(2,1)} %bitcast.24, ...), kind=kOutput, calls=%fused_computation.4 | convolution fusion | flops 20980432896 | bytes 62783488 | tf_op jit(solution)/shard_map/dot_general | solution.py:86
  126.9 19.0 %fusion.45 = bf16[384,2048]{1,0:T(8,128)(2,1)S(1)} fusion(bf16[6656,4096]{1,0:T(8,128)(2,1)} %param.5, bf16[96,3328]{1,0:T(8,128)(2,1)} %bitcast.43, bf16[96,3328]{1,0:T(8,128)(2,1)} %bitcast.42, bf16[96,3328]{1,0:T(8,128)(2,1)} %bitcast.41, bf16[96,3328]{1,0:T(8,128)(2,1)} %bitcast.40, bf16[96,3328]{1,0:T(8,128)(2,1)} %bitcast.39, ...), kind=kOutput, calls=%fused_computation.53 | convolution fusion | flops 10510663680 | bytes 33947648 | tf_op jit(solution)/shard_map/dot_general | solution.py:86
  146.0 19.2 %fusion.48 = bf16[384,2048]{1,0:T(8,128)(2,1)S(1)} fusion(bf16[6656,4096]{1,0:T(8,128)(2,1)} %param.5, bf16[96,3328]{1,0:T(8,128)(2,1)} %bitcast.43, bf16[96,3328]{1,0:T(8,128)(2,1)} %bitcast.42, bf16[96,3328]{1,0:T(8,128)(2,1)} %bitcast.41, bf16[96,3328]{1,0:T(8,128)(2,1)} %bitcast.40, bf16[96,3328]{1,0:T(8,128)(2,1)} %bitcast.39, ...), kind=kOutput, calls=%fused_computation.54 | convolution fusion | flops 10510663680 | bytes 33947648 | tf_op jit(solution)/shard_map/dot_general | solution.py:86
  166.8 1.5 fusion.51
  168.4 1.4 collective-permute-start.7
  170.8 1.4 collective-permute-start.9
  173.0 3.2 %collective-permute-done.7 = bf16[32,4096]{1,0:T(8,128)(2,1)S(1)} collective-permute-done((bf16[32,4096]{1,0:T(8,128)(2,1)S(1)}, bf16[32,4096]{1,0:T(8,128)(2,1)S(1)}, u32[]{:S(2)}, u32[]{:S(2)}) %collective-permute-start.7) | collective-permute-done | bytes 262176 | tf_op jit(solution)/shard_map/ppermute | solution.py:38
  176.3 2.3 collective-permute-start.28
  178.6 17.9 %collective-permute-done.8 = bf16[32,4096]{1,0:T(8,128)(2,1)S(1)} collective-permute-done((bf16[32,4096]{1,0:T(8,128)(2,1)S(1)}, bf16[32,4096]{1,0:T(8,128)(2,1)S(1)}, u32[]{:S(2)}, u32[]{:S(2)}) %collective-permute-start.8) | collective-permute-done | bytes 262176 | tf_op jit(solution)/shard_map/ppermute | solution.py:38
  196.4 6.4 %collective-permute-done.9 = bf16[32,4096]{1,0:T(8,128)(2,1)S(1)} collective-permute-done((bf16[32,4096]{1,0:T(8,128)(2,1)S(1)}, bf16[32,4096]{1,0:T(8,128)(2,1)S(1)}, u32[]{:S(2)}, u32[]{:S(2)}) %collective-permute-start.9) | collective-permute-done | bytes 262176 | tf_op jit(solution)/shard_map/ppermute | solution.py:38
  203.1 5.9 %collective-permute-done.28 = bf16[48,2048]{1,0:T(8,128)(2,1)S(1)} collective-permute-done((bf16[48,2048]{1,0:T(8,128)(2,1)S(1)}, bf16[48,2048]{1,0:T(8,128)(2,1)S(1)}, u32[]{:S(2)}, u32[]{:S(2)}) %collective-permute-start.28) | collective-permute-done | bytes 196640 | tf_op jit(solution)/shard_map/ppermute | solution.py:38
  209.0 7.7 %collective-permute-start.33 = (bf16[48,2048]{1,0:T(8,128)(2,1)S(1)}, bf16[48,2048]{1,0:T(8,128)(2,1)S(1)}, u32[]{:S(2)}, u32[]{:S(2)}) collective-permute-start(bf16[48,2048]{1,0:T(8,128)(2,1)S(1)} %get-tuple-element.21), channel_id=1, source_target_pairs={{0,24},{4,28},{8,0},{12,4},{16,8},{20,12},{24,16},{28,20},{1,25},{... | collective-permute-start | bytes 589832 | tf_op jit(solution)/shard_map/ppermute | solution.py:38
  216.7 3.0 %collective-permute-done.29 = bf16[48,2048]{1,0:T(8,128)(2,1)S(1)} collective-permute-done((bf16[48,2048]{1,0:T(8,128)(2,1)S(1)}, bf16[48,2048]{1,0:T(8,128)(2,1)S(1)}, u32[]{:S(2)}, u32[]{:S(2)}) %collective-permute-start.29) | collective-permute-done | bytes 196640 | tf_op jit(solution)/shard_map/ppermute | solution.py:38
  220.6 1.4 collective-permute-start.19
  222.0 4.0 %collective-permute-done.32 = bf16[48,2048]{1,0:T(8,128)(2,1)S(1)} collective-permute-done((bf16[48,2048]{1,0:T(8,128)(2,1)S(1)}, bf16[48,2048]{1,0:T(8,128)(2,1)S(1)}, u32[]{:S(2)}, u32[]{:S(2)}) %collective-permute-start.32) | collective-permute-done | bytes 196640 | tf_op jit(solution)/shard_map/ppermute | solution.py:38
  225.9 19.1 %collective-permute-done.33 = bf16[48,2048]{1,0:T(8,128)(2,1)S(1)} collective-permute-done((bf16[48,2048]{1,0:T(8,128)(2,1)S(1)}, bf16[48,2048]{1,0:T(8,128)(2,1)S(1)}, u32[]{:S(2)}, u32[]{:S(2)}) %collective-permute-start.33) | collective-permute-done | bytes 196640 | tf_op jit(solution)/shard_map/ppermute | solution.py:38
  245.1 6.1 %collective-permute-done.17 = bf16[48,4096]{1,0:T(8,128)(2,1)S(1)} collective-permute-done((bf16[48,4096]{1,0:T(8,128)(2,1)S(1)}, bf16[48,4096]{1,0:T(8,128)(2,1)S(1)}, u32[]{:S(2)}, u32[]{:S(2)}) %collective-permute-start.17) | collective-permute-done | bytes 393248 | tf_op jit(solution)/shard_map/ppermute | solution.py:38
  251.2 8.4 %collective-permute-done.18 = bf16[48,4096]{1,0:T(8,128)(2,1)S(1)} collective-permute-done((bf16[48,4096]{1,0:T(8,128)(2,1)S(1)}, bf16[48,4096]{1,0:T(8,128)(2,1)S(1)}, u32[]{:S(2)}, u32[]{:S(2)}) %collective-permute-start.18) | collective-permute-done | bytes 393248 | tf_op jit(solution)/shard_map/ppermute | solution.py:38
  259.7 2.2 collective-permute-done.19
  (84 shorter events, 18.4 us)
Async XLA Ops:
  4.2 10.8 %collective-permute-start.3 = (bf16[2,32,3328]{2,1,0:T(8,128)(2,1)S(1)}, bf16[2,32,3328]{2,1,0:T(8,128)(2,1)S(1)}, u32[]{:S(2)}, u32[]{:S(2)}) collective-permute-start(bf16[2,32,3328]{2,1,0:T(8,128)(2,1)S(1)} %slice.49), channel_id=1, source_target_pairs={{0,1},{1,0},{2,3},{3,2},{4,5},{5,4},{6,7},{7,6},{8,9},{9,8},{10,11... | collective-permute-start | bytes 1277960 | tf_op jit(solution)/shard_map/ppermute | solution.py:30
  5.5 19.9 %collective-permute-start.4 = (bf16[2,32,3328]{2,1,0:T(8,128)(2,1)S(1)}, bf16[2,32,3328]{2,1,0:T(8,128)(2,1)S(1)}, u32[]{:S(2)}, u32[]{:S(2)}) collective-permute-start(bf16[2,32,3328]{2,1,0:T(8,128)(2,1)S(1)} %slice.49), channel_id=1, source_target_pairs={{0,2},{1,3},{2,0},{3,1},{4,6},{5,7},{6,4},{7,5},{8,10},{9,11},{10,... | collective-permute-start | bytes 1277960 | tf_op jit(solution)/shard_map/ppermute | solution.py:26
  6.9 18.3 %collective-permute-start.1 = (bf16[2,32,3328]{2,1,0:T(8,128)(2,1)S(1)}, bf16[2,32,3328]{2,1,0:T(8,128)(2,1)}, u32[]{:S(2)}, u32[]{:S(2)}) collective-permute-start(bf16[2,32,3328]{2,1,0:T(8,128)(2,1)S(1)} %slice.48), channel_id=1, source_target_pairs={{0,2},{1,3},{2,0},{3,1},{4,6},{5,7},{6,4},{7,5},{8,10},{9,11},{10,... | collective-permute-start | bytes 1277960 | tf_op jit(solution)/shard_map/ppermute | solution.py:26
  7.1 19.5 %collective-permute-start = (bf16[2,32,3328]{2,1,0:T(8,128)(2,1)S(1)}, bf16[2,32,3328]{2,1,0:T(8,128)(2,1)S(1)}, u32[]{:S(2)}, u32[]{:S(2)}) collective-permute-start(bf16[2,32,3328]{2,1,0:T(8,128)(2,1)S(1)} %slice.48), channel_id=1, source_target_pairs={{0,1},{1,0},{2,3},{3,2},{4,5},{5,4},{6,7},{7,6},{8,9},{9,8},{10,11... | collective-permute-start | bytes 1277960 | tf_op jit(solution)/shard_map/ppermute | solution.py:30
  8.3 30.5 %collective-permute-start.11 = (bf16[2,48,3328]{2,1,0:T(8,128)(2,1)S(1)}, bf16[2,48,3328]{2,1,0:T(8,128)(2,1)}, u32[]{:S(2)}, u32[]{:S(2)}) collective-permute-start(bf16[2,48,3328]{2,1,0:T(8,128)(2,1)S(1)} %get-tuple-element.7), channel_id=1, source_target_pairs={{0,2},{1,3},{2,0},{3,1},{4,6},{5,7},{6,4},{7,5},{8,10},{9,11},{10,... | collective-permute-start | bytes 1916936 | tf_op jit(solution)/shard_map/ppermute | solution.py:26
  14.9 25.1 %collective-permute-start.13 = (bf16[2,48,3328]{2,1,0:T(8,128)(2,1)S(1)}, bf16[2,48,3328]{2,1,0:T(8,128)(2,1)}, u32[]{:S(2)}, u32[]{:S(2)}) collective-permute-start(bf16[2,48,3328]{2,1,0:T(8,128)(2,1)S(1)} %get-tuple-element.9), channel_id=1, source_target_pairs={{0,1},{1,0},{2,3},{3,2},{4,5},{5,4},{6,7},{7,6},{8,9},{9,8},{10,11... | collective-permute-start | bytes 1916936 | tf_op jit(solution)/shard_map/ppermute | solution.py:30
  25.1 26.5 %collective-permute-start.10 = (bf16[2,48,3328]{2,1,0:T(8,128)(2,1)S(1)}, bf16[2,48,3328]{2,1,0:T(8,128)(2,1)S(1)}, u32[]{:S(2)}, u32[]{:S(2)}) collective-permute-start(bf16[2,48,3328]{2,1,0:T(8,128)(2,1)S(1)} %get-tuple-element.7), channel_id=1, source_target_pairs={{0,1},{1,0},{2,3},{3,2},{4,5},{5,4},{6,7},{7,6},{8,9},{9,8},{10,11... | collective-permute-start | bytes 1916936 | tf_op jit(solution)/shard_map/ppermute | solution.py:30
  25.4 27.4 %collective-permute-start.5 = (bf16[2,32,3328]{2,1,0:T(8,128)(2,1)S(1)}, bf16[2,32,3328]{2,1,0:T(8,128)(2,1)}, u32[]{:S(2)}, u32[]{:S(2)}) collective-permute-start(bf16[2,32,3328]{2,1,0:T(8,128)(2,1)S(1)} %collective-permute-done.3), channel_id=1, source_target_pairs={{0,2},{1,3},{2,0},{3,1},{4,6},{5,7},{6,4},{7,5},{8,10},{9,11},{10,... | collective-permute-start | bytes 1277960 | tf_op jit(solution)/shard_map/ppermute | solution.py:26
  26.6 34.1 %collective-permute-start.2 = (bf16[2,32,3328]{2,1,0:T(8,128)(2,1)}, bf16[2,32,3328]{2,1,0:T(8,128)(2,1)}, u32[]{:S(2)}, u32[]{:S(2)}) collective-permute-start(bf16[2,32,3328]{2,1,0:T(8,128)(2,1)} %collective-permute-done.1), channel_id=1, source_target_pairs={{0,1},{1,0},{2,3},{3,2},{4,5},{5,4},{6,7},{7,6},{8,9},{9,8},{10,11... | collective-permute-start | bytes 1277960 | tf_op jit(solution)/shard_map/ppermute | solution.py:30
  38.8 48.4 %collective-permute-start.14 = (bf16[2,48,3328]{2,1,0:T(8,128)(2,1)S(1)}, bf16[2,48,3328]{2,1,0:T(8,128)(2,1)}, u32[]{:S(2)}, u32[]{:S(2)}) collective-permute-start(bf16[2,48,3328]{2,1,0:T(8,128)(2,1)S(1)} %get-tuple-element.9), channel_id=1, source_target_pairs={{0,2},{1,3},{2,0},{3,1},{4,6},{5,7},{6,4},{7,5},{8,10},{9,11},{10,... | collective-permute-start | bytes 1916936 | tf_op jit(solution)/shard_map/ppermute | solution.py:26
  40.0 48.3 %collective-permute-start.21 = (bf16[2,48,3328]{2,1,0:T(8,128)(2,1)}, bf16[2,48,3328]{2,1,0:T(8,128)(2,1)}, u32[]{:S(2)}, u32[]{:S(2)}) collective-permute-start(bf16[2,48,3328]{2,1,0:T(8,128)(2,1)} %get-tuple-element.8), channel_id=1, source_target_pairs={{0,2},{1,3},{2,0},{3,1},{4,6},{5,7},{6,4},{7,5},{8,10},{9,11},{10,... | collective-permute-start | bytes 1916936 | tf_op jit(solution)/shard_map/ppermute | solution.py:26
  51.6 37.0 %collective-permute-start.23 = (bf16[2,48,3328]{2,1,0:T(8,128)(2,1)}, bf16[2,48,3328]{2,1,0:T(8,128)(2,1)}, u32[]{:S(2)}, u32[]{:S(2)}) collective-permute-start(bf16[2,48,3328]{2,1,0:T(8,128)(2,1)} %get-tuple-element.10), channel_id=1, source_target_pairs={{0,1},{1,0},{2,3},{3,2},{4,5},{5,4},{6,7},{7,6},{8,9},{9,8},{10,11... | collective-permute-start | bytes 1916936 | tf_op jit(solution)/shard_map/ppermute | solution.py:30
  52.8 36.1 %collective-permute-start.12 = (bf16[2,48,3328]{2,1,0:T(8,128)(2,1)}, bf16[2,48,3328]{2,1,0:T(8,128)(2,1)}, u32[]{:S(2)}, u32[]{:S(2)}) collective-permute-start(bf16[2,48,3328]{2,1,0:T(8,128)(2,1)} %collective-permute-done.11), channel_id=1, source_target_pairs={{0,1},{1,0},{2,3},{3,2},{4,5},{5,4},{6,7},{7,6},{8,9},{9,8},{10,11... | collective-permute-start | bytes 1916936 | tf_op jit(solution)/shard_map/ppermute | solution.py:30
  60.7 29.4 %collective-permute-start.15 = (bf16[2,48,3328]{2,1,0:T(8,128)(2,1)}, bf16[2,48,3328]{2,1,0:T(8,128)(2,1)}, u32[]{:S(2)}, u32[]{:S(2)}) collective-permute-start(bf16[2,48,3328]{2,1,0:T(8,128)(2,1)} %collective-permute-done.13), channel_id=1, source_target_pairs={{0,2},{1,3},{2,0},{3,1},{4,6},{5,7},{6,4},{7,5},{8,10},{9,11},{10,... | collective-permute-start | bytes 1916936 | tf_op jit(solution)/shard_map/ppermute | solution.py:26
  87.2 39.7 %collective-permute-start.20 = (bf16[2,48,3328]{2,1,0:T(8,128)(2,1)}, bf16[2,48,3328]{2,1,0:T(8,128)(2,1)}, u32[]{:S(2)}, u32[]{:S(2)}) collective-permute-start(bf16[2,48,3328]{2,1,0:T(8,128)(2,1)} %get-tuple-element.8), channel_id=1, source_target_pairs={{0,1},{1,0},{2,3},{3,2},{4,5},{5,4},{6,7},{7,6},{8,9},{9,8},{10,11... | collective-permute-start | bytes 1916936 | tf_op jit(solution)/shard_map/ppermute | solution.py:30
  88.4 38.5 %collective-permute-start.24 = (bf16[2,48,3328]{2,1,0:T(8,128)(2,1)}, bf16[2,48,3328]{2,1,0:T(8,128)(2,1)}, u32[]{:S(2)}, u32[]{:S(2)}) collective-permute-start(bf16[2,48,3328]{2,1,0:T(8,128)(2,1)} %get-tuple-element.10), channel_id=1, source_target_pairs={{0,2},{1,3},{2,0},{3,1},{4,6},{5,7},{6,4},{7,5},{8,10},{9,11},{10,... | collective-permute-start | bytes 1916936 | tf_op jit(solution)/shard_map/ppermute | solution.py:26
  88.6 38.3 %collective-permute-start.22 = (bf16[2,48,3328]{2,1,0:T(8,128)(2,1)}, bf16[2,48,3328]{2,1,0:T(8,128)(2,1)}, u32[]{:S(2)}, u32[]{:S(2)}) collective-permute-start(bf16[2,48,3328]{2,1,0:T(8,128)(2,1)} %collective-permute-done.21), channel_id=1, source_target_pairs={{0,1},{1,0},{2,3},{3,2},{4,5},{5,4},{6,7},{7,6},{8,9},{9,8},{10,11... | collective-permute-start | bytes 1916936 | tf_op jit(solution)/shard_map/ppermute | solution.py:30
  88.9 38.1 %collective-permute-start.25 = (bf16[2,48,3328]{2,1,0:T(8,128)(2,1)}, bf16[2,48,3328]{2,1,0:T(8,128)(2,1)}, u32[]{:S(2)}, u32[]{:S(2)}) collective-permute-start(bf16[2,48,3328]{2,1,0:T(8,128)(2,1)} %collective-permute-done.23), channel_id=1, source_target_pairs={{0,2},{1,3},{2,0},{3,1},{4,6},{5,7},{6,4},{7,5},{8,10},{9,11},{10,... | collective-permute-start | bytes 1916936 | tf_op jit(solution)/shard_map/ppermute | solution.py:26
  90.1 76.2 %collective-permute-start.6 = (bf16[4,32,4096]{2,1,0:T(8,128)(2,1)}, bf16[4,32,4096]{2,1,0:T(8,128)(2,1)}, u32[]{:S(2)}, u32[]{:S(2)}) collective-permute-start(bf16[4,32,4096]{2,1,0:T(8,128)(2,1)} %dynamic-slice_bitcast_fusion.1), channel_id=1, source_target_pairs={{0,4},{4,0},{8,12},{12,8},{16,20},{20,16},{24,28},{28,24},{1,5},{5... | collective-permute-start | bytes 3145736 | tf_op jit(solution)/shard_map/ppermute | solution.py:34
  165.4 54.4 %collective-permute-start.16 = (bf16[4,48,4096]{2,1,0:T(8,128)(2,1)S(1)}, bf16[4,48,4096]{2,1,0:T(8,128)(2,1)S(1)}, u32[]{:S(2)}, u32[]{:S(2)}) collective-permute-start(bf16[4,48,4096]{2,1,0:T(8,128)(2,1)S(1)} %dynamic-slice_bitcast_fusion), channel_id=1, source_target_pairs={{0,4},{4,0},{8,12},{12,8},{16,20},{20,16},{24,28},{28,24},{1,5},{5... | collective-permute-start | bytes 4718600 | tf_op jit(solution)/shard_map/ppermute | solution.py:34
  168.4 7.9 %collective-permute-start.7 = (bf16[32,4096]{1,0:T(8,128)(2,1)S(1)}, bf16[32,4096]{1,0:T(8,128)(2,1)S(1)}, u32[]{:S(2)}, u32[]{:S(2)}) collective-permute-start(bf16[32,4096]{1,0:T(8,128)(2,1)S(1)} %get-tuple-element.14), channel_id=1, source_target_pairs={{0,8},{4,12},{8,16},{12,20},{16,24},{20,28},{24,0},{28,4},{1,9},{5... | collective-permute-start | bytes 786440 | tf_op jit(solution)/shard_map/ppermute | solution.py:38
  169.7 26.7 %collective-permute-start.8 = (bf16[32,4096]{1,0:T(8,128)(2,1)S(1)}, bf16[32,4096]{1,0:T(8,128)(2,1)S(1)}, u32[]{:S(2)}, u32[]{:S(2)}) collective-permute-start(bf16[32,4096]{1,0:T(8,128)(2,1)S(1)} %get-tuple-element.16), channel_id=1, source_target_pairs={{0,16},{4,20},{8,24},{12,28},{16,0},{20,4},{24,8},{28,12},{1,17},{... | collective-permute-start | bytes 786440 | tf_op jit(solution)/shard_map/ppermute | solution.py:38
  170.8 32.0 %collective-permute-start.9 = (bf16[32,4096]{1,0:T(8,128)(2,1)S(1)}, bf16[32,4096]{1,0:T(8,128)(2,1)S(1)}, u32[]{:S(2)}, u32[]{:S(2)}) collective-permute-start(bf16[32,4096]{1,0:T(8,128)(2,1)S(1)} %get-tuple-element.15), channel_id=1, source_target_pairs={{0,24},{4,28},{8,0},{12,4},{16,8},{20,12},{24,16},{28,20},{1,25},{... | collective-permute-start | bytes 786440 | tf_op jit(solution)/shard_map/ppermute | solution.py:38
  172.5 30.4 %collective-permute-start.27 = (bf16[48,2048]{1,0:T(8,128)(2,1)S(1)}, bf16[48,2048]{1,0:T(8,128)(2,1)S(1)}, u32[]{:S(2)}, u32[]{:S(2)}) collective-permute-start(bf16[48,2048]{1,0:T(8,128)(2,1)S(1)} %get-tuple-element.17), channel_id=1, source_target_pairs={{0,8},{4,12},{8,16},{12,20},{16,24},{20,28},{24,0},{28,4},{1,9},{5... | collective-permute-start | bytes 589832 | tf_op jit(solution)/shard_map/ppermute | solution.py:38
  176.3 32.7 %collective-permute-start.28 = (bf16[48,2048]{1,0:T(8,128)(2,1)S(1)}, bf16[48,2048]{1,0:T(8,128)(2,1)S(1)}, u32[]{:S(2)}, u32[]{:S(2)}) collective-permute-start(bf16[48,2048]{1,0:T(8,128)(2,1)S(1)} %get-tuple-element.19), channel_id=1, source_target_pairs={{0,16},{4,20},{8,24},{12,28},{16,0},{20,4},{24,8},{28,12},{1,17},{... | collective-permute-start | bytes 589832 | tf_op jit(solution)/shard_map/ppermute | solution.py:38
  196.4 23.3 %collective-permute-start.29 = (bf16[48,2048]{1,0:T(8,128)(2,1)S(1)}, bf16[48,2048]{1,0:T(8,128)(2,1)S(1)}, u32[]{:S(2)}, u32[]{:S(2)}) collective-permute-start(bf16[48,2048]{1,0:T(8,128)(2,1)S(1)} %get-tuple-element.18), channel_id=1, source_target_pairs={{0,24},{4,28},{8,0},{12,4},{16,8},{20,12},{24,16},{28,20},{1,25},{... | collective-permute-start | bytes 589832 | tf_op jit(solution)/shard_map/ppermute | solution.py:38
  202.8 17.8 %collective-permute-start.31 = (bf16[48,2048]{1,0:T(8,128)(2,1)S(1)}, bf16[48,2048]{1,0:T(8,128)(2,1)S(1)}, u32[]{:S(2)}, u32[]{:S(2)}) collective-permute-start(bf16[48,2048]{1,0:T(8,128)(2,1)S(1)} %get-tuple-element.20), channel_id=1, source_target_pairs={{0,8},{4,12},{8,16},{12,20},{16,24},{20,28},{24,0},{28,4},{1,9},{5... | collective-permute-start | bytes 589832 | tf_op jit(solution)/shard_map/ppermute | solution.py:38
  203.0 23.0 %collective-permute-start.32 = (bf16[48,2048]{1,0:T(8,128)(2,1)S(1)}, bf16[48,2048]{1,0:T(8,128)(2,1)S(1)}, u32[]{:S(2)}, u32[]{:S(2)}) collective-permute-start(bf16[48,2048]{1,0:T(8,128)(2,1)S(1)} %get-tuple-element.22), channel_id=1, source_target_pairs={{0,16},{4,20},{8,24},{12,28},{16,0},{20,4},{24,8},{28,12},{1,17},{... | collective-permute-start | bytes 589832 | tf_op jit(solution)/shard_map/ppermute | solution.py:38
  209.0 36.1 %collective-permute-start.33 = (bf16[48,2048]{1,0:T(8,128)(2,1)S(1)}, bf16[48,2048]{1,0:T(8,128)(2,1)S(1)}, u32[]{:S(2)}, u32[]{:S(2)}) collective-permute-start(bf16[48,2048]{1,0:T(8,128)(2,1)S(1)} %get-tuple-element.21), channel_id=1, source_target_pairs={{0,24},{4,28},{8,0},{12,4},{16,8},{20,12},{24,16},{28,20},{1,25},{... | collective-permute-start | bytes 589832 | tf_op jit(solution)/shard_map/ppermute | solution.py:38
  220.5 30.8 %collective-permute-start.17 = (bf16[48,4096]{1,0:T(8,128)(2,1)S(1)}, bf16[48,4096]{1,0:T(8,128)(2,1)S(1)}, u32[]{:S(2)}, u32[]{:S(2)}) collective-permute-start(bf16[48,4096]{1,0:T(8,128)(2,1)S(1)} %get-tuple-element.11), channel_id=1, source_target_pairs={{0,8},{4,12},{8,16},{12,20},{16,24},{20,28},{24,0},{28,4},{1,9},{5... | collective-permute-start | bytes 1179656 | tf_op jit(solution)/shard_map/ppermute | solution.py:38
  220.5 39.1 %collective-permute-start.18 = (bf16[48,4096]{1,0:T(8,128)(2,1)S(1)}, bf16[48,4096]{1,0:T(8,128)(2,1)S(1)}, u32[]{:S(2)}, u32[]{:S(2)}) collective-permute-start(bf16[48,4096]{1,0:T(8,128)(2,1)S(1)} %get-tuple-element.13), channel_id=1, source_target_pairs={{0,16},{4,20},{8,24},{12,28},{16,0},{20,4},{24,8},{28,12},{1,17},{... | collective-permute-start | bytes 1179656 | tf_op jit(solution)/shard_map/ppermute | solution.py:38
  220.6 41.3 %collective-permute-start.19 = (bf16[48,4096]{1,0:T(8,128)(2,1)S(1)}, bf16[48,4096]{1,0:T(8,128)(2,1)S(1)}, u32[]{:S(2)}, u32[]{:S(2)}) collective-permute-start(bf16[48,4096]{1,0:T(8,128)(2,1)S(1)} %get-tuple-element.12), channel_id=1, source_target_pairs={{0,24},{4,28},{8,0},{12,4},{16,8},{20,12},{24,16},{28,20},{1,25},{... | collective-permute-start | bytes 1179656 | tf_op jit(solution)/shard_map/ppermute | solution.py:38
  (12 other events, 347.4 us)
